TPU v7x, 32 devices: a whole 2x2x4 slice. The times are simulated.
32 devices in a mesh: dp: 8 (over z, y), tensor: 4 (over x, core).
Axes of the slice: x: 2, y: 2, z: 4, core: 2. Of those that a mesh axis runs over, the one named last changes fastest.
Arguments:
- inputs: bfloat16 [8192, 1152], P(('dp', 'tensor')), may hold values from -6 to 6
- segments: int32 [8192], P('dp'), may hold values from 0 to 16, as said below
- w_query: bfloat16 [1152, 1024], P('dp', 'tensor'), may hold values from -0.1875 to 0.1875
- w_key: bfloat16 [1152, 256], P('dp'), may hold values from -0.1875 to 0.1875
- w_value: bfloat16 [1152, 256], P('dp'), may hold values from -0.1875 to 0.1875
- w_out: bfloat16 [1024, 1152], P('tensor', 'dp'), may hold values from -0.375 to 0.375
- g_in: bfloat16 [1152], P('dp'), may hold values from 0.25 to 1.75
- g_attn: bfloat16 [1152], P('dp'), may hold values from 0.25 to 1.75
- g_query: bfloat16 [256], replicated, may hold values from 0.25 to 1.75
- g_key: bfloat16 [256], replicated, may hold values from 0.25 to 1.75
- w_gate: bfloat16 [1152, 6912], P('dp', 'tensor'), may hold values from -0.1875 to 0.1875
- w_up: bfloat16 [1152, 6912], P('dp', 'tensor'), may hold values from -0.1875 to 0.1875
- w_down: bfloat16 [6912, 1152], P('tensor', 'dp'), may hold values from -0.078125 to 0.078125
- g_pre: bfloat16 [1152], P('dp'), may hold values from 0.25 to 1.75
- g_post: bfloat16 [1152], P('dp'), may hold values from 0.25 to 1.75
- cotangent: bfloat16 [8192, 1152], P(('dp', 'tensor')), may hold values from -6 to 6
Outputs:
- output: bfloat16 [8192, 1152], P(('dp', 'tensor'))
- d_inputs: bfloat16 [8192, 1152], P(('dp', 'tensor'))
- grad_query: float32 [1152, 1024], P('dp', 'tensor')
- grad_key: float32 [1152, 256], P(('dp', 'tensor'))
- grad_value: float32 [1152, 256], P(('dp', 'tensor'))
- grad_out: float32 [1024, 1152], P('tensor', 'dp')
- grad_g_in: float32 [1152], P(('dp', 'tensor'))
- grad_g_attn: float32 [1152], P(('dp', 'tensor'))
- grad_g_query: float32 [256], P(('dp', 'tensor'))
- grad_g_key: float32 [256], P(('dp', 'tensor'))
- grad_gate: float32 [1152, 6912], P('dp', 'tensor')
- grad_up: float32 [1152, 6912], P('dp', 'tensor')
- grad_down: float32 [6912, 1152], P('tensor', 'dp')
- grad_g_pre: float32 [1152], P(('dp', 'tensor'))
- grad_g_post: float32 [1152], P(('dp', 'tensor'))
Inputs may be any that keep to these rules, and one draw needn't show every extreme that they name: `segments`: within each block of 1024 rows segment numbers start at 0 and rise by one at the first row of each packed sequence; a sequence starts at every multiple of 512 rows, so none is longer than 512. Every block holds one sequence of exactly 512 rows, and each of its other spans of 512 rows starting at a multiple of 512 holds exactly 16 sequences of uneven lengths.
All inputs are finite; a program needn't handle non-finite values.
Results may differ from a plain program's by a relative error of at most 0.02.
Values may be sent and summed in bfloat16 or wider, within the bound.
A program may use at most 192 MiB of HBM per device.

v0:
```python
from functools import partial

import jax
import jax.numpy as jnp
from jax import lax
from jax.experimental import pallas as pl
from jax.experimental.pallas import tpu as pltpu
from jax.sharding import PartitionSpec as P

HD = 256
SEGMAX = 512
MESH = pl.DeviceIdType.MESH
BF = jnp.bfloat16
F32 = jnp.float32


def ring_pos(dev, n):
    return (1 - dev % 2) * (dev // 2) + (dev % 2) * (n - 1 - dev // 2)


def ring_dev(pos, n):
    high = pos // (n // 2)
    return (1 - high) * (2 * pos) + high * (2 * (n - 1 - pos) + 1)


def barrier(peers):
    sem = pltpu.get_barrier_semaphore()
    for peer in peers:
        pl.semaphore_signal(sem, inc=1, device_id=peer, device_id_type=MESH)
    pl.semaphore_wait(sem, len(peers))


def reach(bias, way, n):
    return n // 2 if bias == way else n // 2 - 1


class Ring:
    def __init__(self, n, parts, send_sem, recv_sem, land=None):
        self.n, self.parts, self.land = n, parts, land
        self.send_sem, self.recv_sem = send_sem, recv_sem
        self.me = lax.axis_index("dp")
        self.pos = ring_pos(self.me, n)
        self.peer = [{"dp": self.dev(1)}, {"dp": self.dev(-1)}]

    def dev(self, offset):
        return ring_dev((self.pos + (offset + self.n) % self.n) % self.n, self.n)

    def reach(self, part, way):
        return reach(part % 2, way, self.n)

    def gather(self, part, way, hop, ahead):
        away = hop - 1 if ahead else hop
        block = self.parts[part](self.dev(-away if way == 0 else away))
        return pltpu.make_async_remote_copy(
            block,
            block,
            self.send_sem.at[part, way, hop - 1],
            self.recv_sem.at[part, way, hop - 1],
            device_id=self.peer[way],
            device_id_type=MESH,
        )

    def gather_step(self, part, way, hop):
        if hop > 1:
            self.gather(part, way, hop - 1, False).wait_recv()
        if hop <= self.reach(part, way):
            self.gather(part, way, hop, True).start()

    def gather_sends_done(self, part):
        for way in range(2):
            for hop in range(1, self.reach(part, way) + 1):
                self.gather(part, way, hop, True).wait_send()

    def target(self, part, way, hop):
        away = self.reach(part, way) - hop + 1
        return self.dev(away if way == 0 else -away)

    def slot(self, part, way, hop):
        return self.land(part, hop - 1 + (self.reach(part, 0) if way else 0))

    def reduce(self, part, way, hop):
        return pltpu.make_async_remote_copy(
            self.parts[part](self.target(part, way, hop)),
            self.slot(part, way, hop),
            self.send_sem.at[part, way, hop - 1],
            self.recv_sem.at[part, way, hop - 1],
            device_id=self.peer[way],
            device_id_type=MESH,
        )

    def reduce_step(self, part, way, hop):
        if hop > self.reach(part, way):
            return
        if hop > 1:
            self.reduce(part, way, hop - 1).wait_recv()
            own = self.parts[part](self.target(part, way, hop))
            came = self.slot(part, way, hop - 1)
            own[...] = (own[...].astype(F32) + came[...].astype(F32)).astype(BF)
        self.reduce(part, way, hop).start()

    def reduce_end(self, part):
        total = self.parts[part](self.me)[...].astype(F32)
        for way in range(2):
            last = self.reach(part, way)
            self.reduce(part, way, last).wait_recv()
            total = total + self.slot(part, way, last)[...].astype(F32)
        return total

    def reduce_sends_done(self, part):
        for way in range(2):
            for hop in range(1, self.reach(part, way) + 1):
                self.reduce(part, way, hop).wait_send()


def part_views(attn, attn_cut, ffn=None, ffn_cut=()):
    views = []
    for low, high in attn_cut:
        views.append(lambda b, low=low, high=high: attn.at[b, :, pl.ds(low, high - low)])
    for chunk in range(0 if ffn is None else ffn.shape[0]):
        for low, high in ffn_cut:
            views.append(
                lambda b, c=chunk, low=low, high=high: ffn.at[c, b, :, pl.ds(low, high - low)]
            )
    return views


def halves(cols, step=128):
    mid = cols // 2 // step * step
    return ((0, mid), (mid, cols))


def gather_kernel(n, attn_ref, ffn_ref, attn_out, ffn_out, local_sem, send_sem, recv_sem):
    parts = part_views(attn_out, halves(attn_ref.shape[-1]), ffn_out, halves(ffn_ref.shape[-1]))
    ring = Ring(n, parts, send_sem, recv_sem)
    mine = [
        pltpu.make_async_copy(attn_ref, attn_out.at[ring.me], local_sem.at[0]),
        pltpu.make_async_copy(ffn_ref, ffn_out.at[:, ring.me], local_sem.at[1]),
    ]
    for copy in mine:
        copy.start()
    barrier(ring.peer)
    for copy in mine:
        copy.wait()
    width = 4
    for low in range(0, len(parts), width):
        for hop in range(1, n // 2 + 2):
            for part in range(low, min(low + width, len(parts))):
                for way in range(2):
                    if hop <= ring.reach(part, way) + 1:
                        ring.gather_step(part, way, hop)
    for part in range(len(parts)):
        ring.gather_sends_done(part)


def reduce_kernel(n, attn_ref, ffn_ref, attn_out, ffn_out, attn_buf, ffn_buf, attn_land, ffn_land, local_sem, send_sem, recv_sem):
    acut, fcut = halves(attn_ref.shape[-1]), halves(ffn_ref.shape[-1])
    parts = part_views(attn_buf, acut, ffn_buf, fcut)
    landing = part_views(attn_land, acut, ffn_land, fcut)
    ring = Ring(n, parts, send_sem, recv_sem, lambda part, slot: landing[part](slot))
    load = [
        pltpu.make_async_copy(attn_ref, attn_buf, local_sem.at[0]),
        pltpu.make_async_copy(ffn_ref, ffn_buf, local_sem.at[1]),
    ]
    for copy in load:
        copy.start()
    barrier(ring.peer)
    for copy in load:
        copy.wait()
    width = 4
    for low in range(0, len(parts), width):
        for hop in range(1, n // 2 + 1):
            for part in range(low, min(low + width, len(parts))):
                for way in range(2):
                    ring.reduce_step(part, way, hop)
        for part in range(low, min(low + width, len(parts))):
            total = ring.reduce_end(part)
            if part < 2:
                attn_out[:, acut[part][0] : acut[part][1]] = total
            else:
                cut = fcut[part % 2]
                ffn_out[part // 2 - 1, :, cut[0] : cut[1]] = total
    for part in range(len(parts)):
        ring.reduce_sends_done(part)


VMEM_LIMIT = 60 * 2**20


def vmem_specs(count):
    return [pl.BlockSpec(memory_space=pltpu.VMEM)] * count


def any_specs(count):
    return [pl.BlockSpec(memory_space=pl.ANY)] * count


def ring_gather(n, attn, ffn):
    chunks = ffn.shape[0]
    sems = pltpu.SemaphoreType.DMA((2 * (chunks + 1), 2, n // 2))
    return pl.pallas_call(
        partial(gather_kernel, n),
        out_shape=(
            jax.ShapeDtypeStruct((n,) + attn.shape, BF),
            jax.ShapeDtypeStruct((chunks, n) + ffn.shape[1:], BF),
        ),
        in_specs=any_specs(2),
        out_specs=vmem_specs(2),
        scratch_shapes=[pltpu.SemaphoreType.DMA((2,)), sems, sems],
        compiler_params=pltpu.CompilerParams(
            collective_id=0, has_side_effects=True, vmem_limit_bytes=VMEM_LIMIT
        ),
    )(attn, ffn)


def ring_reduce(n, attn, ffn):
    chunks, _, rows, cols = ffn.shape
    sems = pltpu.SemaphoreType.DMA((2 * (chunks + 1), 2, n // 2))
    return pl.pallas_call(
        partial(reduce_kernel, n),
        out_shape=(
            jax.ShapeDtypeStruct(attn.shape[1:], F32),
            jax.ShapeDtypeStruct((chunks, rows, cols), F32),
        ),
        in_specs=any_specs(2),
        out_specs=vmem_specs(2),
        scratch_shapes=[
            pltpu.VMEM(attn.shape, BF),
            pltpu.VMEM(ffn.shape, BF),
            pltpu.VMEM((n - 1,) + attn.shape[1:], BF),
            pltpu.VMEM((chunks, n - 1, rows, cols), BF),
            pltpu.SemaphoreType.DMA((2,)),
            sems,
            sems,
        ],
        compiler_params=pltpu.CompilerParams(
            collective_id=1, has_side_effects=True, vmem_limit_bytes=VMEM_LIMIT
        ),
    )(attn, ffn)


CHUNK = 256


def pack_rows(array, rows):
    return jnp.pad(array, ((0, rows - array.shape[0]), (0, 0)))


def pack_ffn(gate, up, down_t, rows, step=CHUNK):
    width = gate.shape[1]
    chunks = -(-width // step)
    chunks += chunks % 2 if step != CHUNK else 0

    def cut(array):
        array = jnp.pad(array, ((0, rows - array.shape[0]), (0, chunks * step - width)))
        return array.reshape(rows, chunks, step).transpose(1, 0, 2)

    return jnp.concatenate([cut(gate), cut(up), cut(down_t)], axis=2)


def unpack_ffn(packed, width):
    chunks, rows = packed.shape[:2]
    out = []
    for k in range(3):
        piece = packed[:, :, k * CHUNK : (k + 1) * CHUNK]
        out.append(piece.transpose(1, 0, 2).reshape(rows, chunks * CHUNK)[:, :width])
    return out


def pack_blocks(array, n, rows):
    depth = array.shape[0] // n
    return jnp.pad(array.reshape(n, depth, -1), ((0, 0), (0, rows - depth), (0, 0)))


EPSILON = 1e-06
THETA = 1000000.0
NEG_LARGE = -1e30


def rms_scale(values, gain_vec):
    inverse = lax.rsqrt(jnp.mean(values * values, axis=-1, keepdims=True) + EPSILON)
    return values * inverse * gain_vec


def gelu_product(gate_proj, up_proj):
    return jax.nn.gelu(gate_proj, approximate=True) * up_proj


def rows_product(left, right):
    return lax.dot_general(
        left, right, (((0,), (0,)), ((), ())), preferred_element_type=jnp.float32
    )


def cols_product(left, right):
    return lax.dot_general(
        left, right, (((1,), (1,)), ((), ())), preferred_element_type=jnp.float32
    )


def plain_product(left, right):
    return jnp.dot(left, right, preferred_element_type=jnp.float32)


def rotary_tables(segments):
    count = segments.shape[0]
    row_index = jnp.arange(count, dtype=jnp.int32)
    previous = jnp.concatenate([jnp.full((1,), -1, jnp.int32), segments[:-1]])
    starts = jnp.where(segments != previous, row_index, jnp.zeros_like(row_index))
    seq_start = lax.cummax(starts, axis=0)
    position = (row_index - seq_start).astype(jnp.float32)
    half_width = HD // 2
    exponent = -2.0 * jnp.arange(half_width, dtype=jnp.float32) / HD
    inverse = jnp.power(jnp.float32(THETA), exponent)
    angles = position[:, None] * inverse[None, :]
    cosine = jnp.concatenate([jnp.cos(angles), jnp.cos(angles)], axis=1)
    sine_tab = jnp.concatenate([jnp.sin(angles), jnp.sin(angles)], axis=1)
    return (cosine, sine_tab)


def prepare(projection, gain_vec, cosine, sine_tab):
    normed = rms_scale(projection, gain_vec)
    half_width = HD // 2
    turned = jnp.concatenate([-normed[..., half_width:], normed[..., :half_width]], axis=-1)
    return normed * cosine[:, None, :] + turned * sine_tab[:, None, :]


def visible(segments):
    tile_count = segments.shape[0] // SEGMAX
    seg_tiles = segments.reshape(tile_count, SEGMAX)
    offsets = jnp.arange(SEGMAX, dtype=jnp.int32)
    same = seg_tiles[:, :, None] == seg_tiles[:, None, :]
    return same & (offsets[:, None] >= offsets[None, :])


def tile_scores(query_tiles, key_tiles, segments):
    head_width = key_tiles.shape[-1]
    scores = jnp.einsum(
        "tqhd,tkd->thqk", query_tiles, key_tiles, preferred_element_type=jnp.float32
    ) * head_width ** (-0.5)
    return jnp.where(visible(segments)[:, None], scores, NEG_LARGE)


def attend(query_ready, key_ready, value_b, segments):
    row_count, head_count, head_width = query_ready.shape
    tile_count = row_count // SEGMAX
    query_tiles = query_ready.reshape(tile_count, SEGMAX, head_count, head_width)
    key_tiles = key_ready.reshape(tile_count, SEGMAX, head_width)
    value_tiles = value_b.reshape(tile_count, SEGMAX, head_width)
    scores = tile_scores(query_tiles, key_tiles, segments)
    row_max = jnp.max(scores, axis=-1, keepdims=True)
    row_total = jnp.sum(jnp.exp(scores - row_max), axis=-1, keepdims=True)
    log_total = row_max + jnp.log(row_total)
    probs = jnp.exp(scores - log_total).astype(jnp.bfloat16)
    attended = jnp.einsum("thqk,tkd->tqhd", probs, value_tiles, preferred_element_type=jnp.float32)
    return (attended.reshape(row_count, head_count * head_width).astype(jnp.bfloat16), log_total)


def attend_back(query_ready, key_ready, value_b, segments, log_total, d_attended):
    row_count, head_count, head_width = query_ready.shape
    tile_count = row_count // SEGMAX
    query_tiles = query_ready.reshape(tile_count, SEGMAX, head_count, head_width)
    key_tiles = key_ready.reshape(tile_count, SEGMAX, head_width)
    value_tiles = value_b.reshape(tile_count, SEGMAX, head_width)
    grad_tiles = d_attended.reshape(tile_count, SEGMAX, head_count, head_width)
    scores = tile_scores(query_tiles, key_tiles, segments)
    prob_vals = jnp.exp(scores - log_total)
    prob_b = prob_vals.astype(jnp.bfloat16)
    d_value = jnp.einsum(
        "thqk,tqhd->tkd", prob_b, grad_tiles, preferred_element_type=jnp.float32
    ).reshape(row_count, head_width)
    d_probs = jnp.einsum(
        "tqhd,tkd->thqk", grad_tiles, value_tiles, preferred_element_type=jnp.float32
    )
    row_delta = jnp.sum(prob_vals * d_probs, axis=-1, keepdims=True)
    d_scores = (prob_vals * (d_probs - row_delta) * head_width ** (-0.5)).astype(jnp.bfloat16)
    d_query = jnp.einsum(
        "thqk,tkd->tqhd", d_scores, key_tiles, preferred_element_type=jnp.float32
    ).reshape(row_count, head_count, head_width)
    d_key = jnp.einsum(
        "thqk,tqhd->tkd", d_scores, query_tiles, preferred_element_type=jnp.float32
    ).reshape(row_count, head_width)
    return (d_query, d_key, d_value)


def local(
    inputs,
    segments,
    w_query,
    w_key,
    w_value,
    w_out,
    g_in,
    g_attn,
    g_query,
    g_key,
    w_gate,
    w_up,
    w_down,
    g_pre,
    g_post,
    cotangent,
):
    n = lax.axis_size("dp")
    depth = w_query.shape[0]
    rows = -(-depth // 16) * 16
    width = w_gate.shape[1]
    gains = jnp.stack([g_in, g_attn, g_pre, g_post], axis=1)
    attn_pack = jnp.concatenate(
        [w_query, w_key, w_value, w_out.T, jnp.pad(gains, ((0, 0), (0, 124)))], axis=1
    )
    attn_all, ffn_all = ring_gather(
        n, pack_rows(attn_pack, rows), pack_ffn(w_gate, w_up, w_down.T, rows)
    )
    attn_all = attn_all[:, :depth].reshape(n * depth, -1)
    ffn_all = ffn_all[:, :, :depth].reshape(ffn_all.shape[0], n * depth, -1)
    wq_full, wk_full, wv_full, wo_t = (attn_all[:, k * HD : (k + 1) * HD] for k in range(4))
    wo_full = wo_t.T
    gin_full, gattn_full, gpre_full, gpost_full = (attn_all[:, 4 * HD + k] for k in range(4))
    wg_full, wu_full, wd_t = unpack_ffn(ffn_all, width)
    wd_full = wd_t.T
    gain_in = gin_full.astype(jnp.float32)
    gain_attn = gattn_full.astype(jnp.float32)
    gain_query = g_query.astype(jnp.float32)
    gain_key = g_key.astype(jnp.float32)
    cosine, sine_tab = rotary_tables(segments)
    inputs_f = inputs.astype(jnp.float32)
    normed_shard = rms_scale(inputs_f, gain_in).astype(jnp.bfloat16)
    normed_in = lax.all_gather(normed_shard, "tensor", axis=0, tiled=True)
    row_count = normed_in.shape[0]
    head_count = wq_full.shape[1] // HD
    key_proj = plain_product(normed_in, wk_full)
    value_b = plain_product(normed_in, wv_full).astype(jnp.bfloat16)
    key_ready = prepare(key_proj[:, None, :], gain_key, cosine, sine_tab)[:, 0, :].astype(
        jnp.bfloat16
    )
    query_proj = plain_product(normed_in, wq_full).reshape(row_count, head_count, HD)
    query_ready = prepare(query_proj, gain_query, cosine, sine_tab).astype(jnp.bfloat16)
    attended, log_total = attend(query_ready, key_ready, value_b, segments)
    projected = lax.psum_scatter(
        plain_product(attended, wo_full), "tensor", scatter_dimension=0, tiled=True
    )
    residual_mid = inputs_f + rms_scale(projected, gain_attn)
    gain_pre = gpre_full.astype(jnp.float32)
    gain_post = gpost_full.astype(jnp.float32)
    normed_mid = lax.all_gather(
        rms_scale(residual_mid, gain_pre).astype(jnp.bfloat16), "tensor", axis=0, tiled=True
    )
    gate_proj = plain_product(normed_mid, wg_full)
    up_proj = plain_product(normed_mid, wu_full)
    hidden = gelu_product(gate_proj, up_proj).astype(jnp.bfloat16)
    feed = lax.psum_scatter(
        plain_product(hidden, wd_full), "tensor", scatter_dimension=0, tiled=True
    )
    output = (residual_mid + rms_scale(feed, gain_post)).astype(jnp.bfloat16)
    wg_back, wu_back, wd_back = wg_full, wu_full, wd_full
    grad_output = cotangent.astype(jnp.float32)
    d_feed_f, grad_g_post = jax.vjp(rms_scale, feed, gain_post)[1](grad_output)
    d_feed = lax.all_gather(d_feed_f.astype(jnp.bfloat16), "tensor", axis=0, tiled=True)
    d_hidden = cols_product(d_feed, wd_back)
    d_gate_f, d_up_f = jax.vjp(gelu_product, gate_proj, up_proj)[1](d_hidden)
    d_gate = d_gate_f.astype(jnp.bfloat16)
    d_up = d_up_f.astype(jnp.bfloat16)
    grad_gate = rows_product(normed_mid, d_gate)
    grad_up = rows_product(normed_mid, d_up)
    d_normed_mid = lax.psum_scatter(
        cols_product(d_gate, wg_back) + cols_product(d_up, wu_back),
        "tensor",
        scatter_dimension=0,
        tiled=True,
    )
    d_mid_n, grad_g_pre = jax.vjp(rms_scale, residual_mid, gain_pre)[1](d_normed_mid)
    d_mid = grad_output + d_mid_n
    d_proj_f, grad_g_attn = jax.vjp(rms_scale, projected, gain_attn)[1](d_mid)
    wq_back, wk_back, wv_back, wo_back = wq_full, wk_full, wv_full, wo_full
    d_proj = lax.all_gather(d_proj_f.astype(jnp.bfloat16), "tensor", axis=0, tiled=True)
    d_attended = cols_product(d_proj, wo_back).astype(jnp.bfloat16)
    d_query_ready, d_key_ready, d_value_f = attend_back(
        query_ready, key_ready, value_b, segments, log_total, d_attended
    )
    rotate_fn = partial(prepare, cosine=cosine, sine_tab=sine_tab)
    d_query_f, grad_g_query = jax.vjp(rotate_fn, query_proj, gain_query)[1](d_query_ready)
    d_key_f, grad_g_key = jax.vjp(rotate_fn, key_proj[:, None, :], gain_key)[1](
        d_key_ready[:, None, :]
    )
    d_query = d_query_f.reshape(row_count, head_count * HD).astype(jnp.bfloat16)
    d_key = d_key_f[:, 0, :].astype(jnp.bfloat16)
    d_value = d_value_f.astype(jnp.bfloat16)
    grad_query = rows_product(normed_in, d_query)
    grad_key = rows_product(normed_in, d_key)
    grad_value = rows_product(normed_in, d_value)
    d_normed_terms = (
        cols_product(d_query, wq_back)
        + cols_product(d_key, wk_back)
        + cols_product(d_value, wv_back)
    )
    d_normed_in = lax.psum_scatter(
        d_normed_terms.astype(jnp.bfloat16), "tensor", scatter_dimension=0, tiled=True
    ).astype(jnp.float32)
    d_in_n, grad_g_in = jax.vjp(rms_scale, inputs_f, gain_in)[1](d_normed_in)
    d_inputs = (d_mid + d_in_n).astype(jnp.bfloat16)
    attn_part = jnp.concatenate(
        [grad_query, grad_key, grad_value, rows_product(d_proj, attended)], axis=1
    ).astype(BF)
    attn_part = pack_blocks(attn_part, n, rows)
    ffn_part = pack_ffn(
        grad_gate.astype(BF), grad_up.astype(BF), rows_product(d_feed, hidden).astype(BF), n * depth
    )
    ffn_part = jax.vmap(lambda a: pack_blocks(a, n, rows))(ffn_part)
    attn_sum, ffn_sum = ring_reduce(n, attn_part, ffn_part)
    attn_sum, ffn_sum = attn_sum[:depth], ffn_sum[:, :depth]
    sum_gate, sum_up, sum_down_t = unpack_ffn(ffn_sum, width)
    split_grads = (
        attn_sum[:, :HD],
        attn_sum[:, 3 * HD : 4 * HD].T,
        sum_gate,
        sum_up,
        sum_down_t.T,
    )
    sum_key, sum_value = attn_sum[:, HD : 2 * HD], attn_sum[:, 2 * HD : 3 * HD]
    shared = (
        lax.psum_scatter(sum_key, "tensor", scatter_dimension=0, tiled=True),
        lax.psum_scatter(sum_value, "tensor", scatter_dimension=0, tiled=True),
        lax.psum_scatter(grad_g_in, ("dp", "tensor"), scatter_dimension=0, tiled=True),
        lax.psum_scatter(grad_g_attn, ("dp", "tensor"), scatter_dimension=0, tiled=True),
        lax.psum_scatter(grad_g_pre, ("dp", "tensor"), scatter_dimension=0, tiled=True),
        lax.psum_scatter(grad_g_post, ("dp", "tensor"), scatter_dimension=0, tiled=True),
        lax.psum_scatter(grad_g_query, ("dp", "tensor"), scatter_dimension=0, tiled=True),
        lax.psum_scatter(grad_g_key, ("dp", "tensor"), scatter_dimension=0, tiled=True),
    )
    return (
        output,
        d_inputs,
        split_grads[0],
        shared[0],
        shared[1],
        split_grads[1],
        shared[2],
        shared[3],
        shared[6],
        shared[7],
        split_grads[2],
        split_grads[3],
        split_grads[4],
        shared[4],
        shared[5],
    )


SCALE = HD**-0.5
ROOT = 0.7978845608028654
CUBIC = 0.044715


def dot_nn(a, b):
    return jnp.dot(a, b, preferred_element_type=F32)


def dot_nt(a, b):
    return lax.dot_general(a, b, (((1,), (1,)), ((), ())), preferred_element_type=F32)


def dot_tn(a, b):
    return lax.dot_general(a, b, (((0,), (0,)), ((), ())), preferred_element_type=F32)


def inverse_rms(values):
    return lax.rsqrt(jnp.mean(values * values, axis=-1, keepdims=True) + EPSILON)


def rms_back(values, gain_vec, grad):
    inverse = inverse_rms(values)
    unit = values * inverse
    scaled = grad * gain_vec
    back = inverse * (scaled - unit * jnp.mean(scaled * unit, axis=-1, keepdims=True))
    return back, grad * unit


def gelu_parts(gate):
    bent = jnp.tanh(ROOT * (gate + CUBIC * gate * gate * gate))
    return 0.5 * gate * (1.0 + bent), bent


class Quad:
    def __init__(self, part, near, far, gather_sems, reduce_sems):
        self.me = lax.axis_index("tensor")
        self.twin = self.me + 1 - 2 * (self.me % 2)
        self.across = (self.me + 2) % 4
        self.corner = (self.twin + 2) % 4
        self.part, self.near, self.far = part, near, far
        self.gather_sems, self.reduce_sems = gather_sems, reduce_sems

    def copy(self, src, dst, sems, use, k, peer):
        return pltpu.make_async_remote_copy(
            src,
            dst,
            sems[0].at[use, k],
            sems[1].at[use, k],
            device_id={"tensor": peer},
            device_id_type=MESH,
        )

    def gather(self, use, k, buf):
        place = self.across if k == 2 else self.me
        block = buf(place) if callable(buf) else buf.at[place]
        peer = self.across if k == 1 else self.twin
        return self.copy(block, block, self.gather_sems, use, k, peer)

    def gather_start(self, use, buf):
        self.gather(use, 1, buf).start()
        self.gather(use, 0, buf).start()

    def gather_relay(self, use, buf):
        self.gather(use, 1, buf).wait_recv()
        self.gather(use, 2, buf).start()

    def gather_end(self, use, buf):
        self.gather(use, 0, buf).wait_recv()
        self.gather(use, 2, buf).wait_recv()
        for k in range(3):
            self.gather(use, k, buf).wait_send()

    def reduce(self, use, k):
        block = self.part.at[(self.twin, self.corner, self.across)[k]]
        land = self.far if k == 2 else self.near.at[k]
        peer = self.across if k == 2 else self.twin
        return self.copy(block, land, self.reduce_sems, use, k, peer)

    def reduce_start(self, use):
        self.reduce(use, 1).start()
        self.reduce(use, 0).start()

    def reduce_relay(self, use):
        self.reduce(use, 1).wait_recv()
        for low in range(0, self.part.shape[1], 64):
            rows = pl.ds(low, 64)
            total = self.part[self.across, rows].astype(F32) + self.near[1, rows].astype(F32)
            self.part[self.across, rows] = total.astype(BF)
        self.reduce(use, 2).start()

    def reduce_end(self, use):
        self.reduce(use, 0).wait_recv()
        self.reduce(use, 2).wait_recv()
        for k in range(3):
            self.reduce(use, k).wait_send()


class Octet:
    def __init__(self, part, near, far, bend, gather_sems, reduce_sems):
        tensor, dp = lax.axis_index("tensor"), lax.axis_index("dp")
        z = dp // 2
        self.low, self.x, self.core = z % 2, tensor // 2, tensor % 2
        self.twin = {"tensor": tensor + 1 - 2 * self.core}
        self.across = {"tensor": (tensor + 2) % 4}
        self.pair = {"dp": dp + 2 - 4 * self.low}
        self.part, self.near, self.far, self.bend = part, near, far, bend
        self.gather_sems, self.reduce_sems = gather_sems, reduce_sems

    def block(self, p, other=0):
        core = (self.core + other) % 2
        return (self.low + p // 2) % 2 * 4 + (self.x + p % 2) % 2 * 2 + core

    def copy(self, src, dst, sems, use, k, peer):
        return pltpu.make_async_remote_copy(
            src, dst, sems[0].at[use, k], sems[1].at[use, k], device_id=peer, device_id_type=MESH
        )

    def gather(self, use, k, buf, come=False):
        half = buf.shape[1] // 2
        if k < 2:
            place, peer = (k + 1 if come else 0), (self.across, self.pair)[k]
            ref = buf.at[self.block(place)]
        elif k < 6:
            ref = buf.at[self.block(k - 2, 1 if come else 0)]
            peer = self.twin
        else:
            place = 3 if come else k - 5
            ref = buf.at[self.block(place), pl.ds((k - 6) * half, half)]
            peer = (self.pair, self.across)[k - 6]
        return self.copy(ref, ref, self.gather_sems, use, k, peer)

    def gather_start(self, use, buf):
        for k in range(3):
            self.gather(use, k, buf).start()

    def gather_relay(self, use, buf, k):
        self.gather(use, k, buf, True).wait_recv()
        self.gather(use, 6 + k, buf).start()
        self.gather(use, 3 + k, buf).start()

    def gather_corner(self, use, buf):
        for k in (6, 7):
            self.gather(use, k, buf, True).wait_recv()
        self.gather(use, 5, buf).start()

    def gather_end(self, use, buf):
        for k in range(2, 6):
            self.gather(use, k, buf, True).wait_recv()
        for k in range(8):
            self.gather(use, k, buf).wait_send()

    def reduce(self, use, k):
        half = self.part.shape[1] // 2
        if k < 4:
            return self.copy(
                self.part.at[self.block(k, 1)], self.near.at[k], self.reduce_sems, use, k, self.twin
            )
        peer = (self.across, self.pair)[k % 2]
        if k < 6:
            src, dst = self.part.at[self.block(3), pl.ds((k - 4) * half, half)], self.bend.at[k - 4]
        else:
            src, dst = self.part.at[self.block(k - 5)], self.far.at[k - 6]
        return self.copy(src, dst, self.reduce_sems, use, k, peer)

    def add(self, place, low, count, came):
        step = 32

        def body(i, _):
            at = pl.multiple_of(i * step, step)
            rows = pl.ds(low + at, step)
            total = self.part[self.block(place), rows].astype(F32) + came[pl.ds(at, step)].astype(F32)
            self.part[self.block(place), rows] = total.astype(BF)
            return 0

        lax.fori_loop(0, count // step, body, 0)

    def reduce_near(self, use, place):
        self.reduce(use, place).wait_recv()
        self.add(place, 0, self.part.shape[1], self.near.at[place])

    def reduce_relay(self, use):
        half = self.part.shape[1] // 2
        for k in range(2):
            self.reduce(use, 4 + k).wait_recv()
            self.add(2 - k, k * half, half, self.bend.at[k])
            self.reduce(use, 7 - k).start()

    def reduce_after(self, use, i):
        for k in range(4):
            pl.when(i == 6 - 2 * k)(lambda k=k: self.reduce(use, k).start())
        for k in (1, 2):
            pl.when(i == 7 - 2 * k)(lambda k=k: self.reduce_near(use, k))
        pl.when(i == 6)(lambda: self.reduce_relay(use))

        @pl.when(i == 1)
        def _():
            self.reduce_near(use, 3)
            self.reduce(use, 4).start()
            self.reduce(use, 5).start()

    @staticmethod
    def arrival(j):
        a, b = j // 2, j % 2
        up = (a + 1) // 2
        mid = up * (2 - up)
        return up + mid * b + a // 3, (1 - mid) * b + mid * (a // 2)

    def gather_before(self, use, buf, j):
        for at, k in ((1, 2), (4, 3), (5, 4), (7, 5)):
            pl.when(j == at)(lambda k=k: self.gather(use, k, buf, True).wait_recv())

        @pl.when(j == 2)
        def _():
            self.gather_relay(use, buf, 0)
            self.gather_relay(use, buf, 1)

        pl.when(j == 6)(lambda: self.gather_corner(use, buf))

    def gather_sends_done(self, use, buf):
        for k in range(8):
            self.gather(use, k, buf).wait_send()

    def reduce_end(self, use):
        for k in (0, 6, 7):
            self.reduce(use, k).wait_recv()
        for k in range(8):
            self.reduce(use, k).wait_send()


class Columns:
    def __init__(self, ffn, other, land, gather_sems, reduce_sems):
        dp = lax.axis_index("dp")
        z, y = dp // 2, dp % 2
        self.low = z % 2
        self.inner = z * (3 - z) > 0
        self.outer = z * (3 - z) < 1
        ranks = (z, z + 1 - 2 * (z % 2), (z + 2) % 4, 3 - z)
        self.mine = [rank * 2 + y for rank in ranks]
        self.theirs = [rank * 2 + 1 - y for rank in ranks]
        self.ffn, self.other, self.land = ffn, other, land
        self.gather_sems, self.reduce_sems = gather_sems, reduce_sems

    def copy(self, src, dst, sems, u, send, recv, peer):
        return pltpu.make_async_remote_copy(
            src,
            dst,
            sems[0].at[u, send],
            sems[1].at[u, recv],
            device_id={"dp": peer},
            device_id_type=MESH,
        )

    def gather(self, u, k):
        own = self.ffn.at[u, self.mine[0]]
        sems = self.gather_sems
        if k == 0:
            return self.copy(own, own, sems, u, 0, 0, self.mine[2])
        if k == 1:
            return self.copy(self.other.at[u], own, sems, u, 1, 1, self.mine[1])
        if k == 2:
            return self.copy(self.other.at[u], own, sems, u, 2, 2, self.mine[3])
        if k == 3:
            block = self.ffn.at[u, self.mine[1]]
            return self.copy(block, block, sems, u, 3, 2, self.mine[2])
        block = self.ffn.at[u, self.mine[k - 4]]
        return self.copy(block, block, sems, u, k, k, self.theirs[0])

    def come(self, u, k):
        place = self.theirs[k - 4] if k >= 4 else self.mine[(2, 1, 3)[k]]
        block = self.ffn.at[u, place]
        self.copy(block, block, self.gather_sems, u, k, k, place).wait_recv()

    def gather_step(self, u, step):
        if step == 0:
            self.gather(u, 0).start()
            self.gather(u, 1).start()
            pl.when(self.inner)(lambda: self.gather(u, 2).start())
            self.gather(u, 4).start()
        elif step == 1:
            self.come(u, 1)
            pl.when(self.inner)(lambda: self.gather(u, 3).start())
            self.gather(u, 5).start()
        elif step == 2:
            self.come(u, 0)
            self.gather(u, 6).start()
        elif step == 3:
            self.come(u, 2)
            self.gather(u, 7).start()
        else:
            for k in range(4, 8):
                self.come(u, k)

    def gather_sends_done(self, u):
        for k in (0, 1, 4, 5, 6, 7):
            self.gather(u, k).wait_send()

        @pl.when(self.inner)
        def _():
            self.gather(u, 2).wait_send()
            self.gather(u, 3).wait_send()

    def piece(self, item, place):
        unit, count, lane, lanes = item[1:]
        return self.ffn.at[pl.ds(unit, count), place, :, pl.ds(lane, lanes)]

    def reduce(self, item, k):
        if k < 4:
            place, peer = self.theirs[k], self.theirs[0]
        else:
            place = self.mine[(2, 1, 3, 3)[k - 4]]
            peer = self.mine[(2, 1, 3, 2)[k - 4]]
        unit, count, lane, lanes = item[1:]
        land = self.land.at[pl.ds(unit, count), k, :, pl.ds(lane, lanes)]
        return self.copy(
            self.piece(item, place), land, self.reduce_sems, item[0], min(k, 6), k, peer
        )

    def came(self, item, k):
        unit, count, lane, lanes = item[1:]
        return [
            self.land[u, k, :, lane : lane + lanes].astype(F32) for u in range(unit, unit + count)
        ]

    def own(self, item, place):
        unit, count, lane, lanes = item[1:]
        return [
            self.ffn.at[u, self.mine[place], :, pl.ds(lane, lanes)]
            for u in range(unit, unit + count)
        ]

    def add(self, item, place, k):
        self.reduce(item, k).wait_recv()
        for own, came in zip(self.own(item, place), self.came(item, k), strict=True):
            own[...] = (own[...].astype(F32) + came).astype(BF)

    def reduce_step(self, item, step):
        if step == 0:
            for k in (3, 2, 1, 0):
                self.reduce(item, k).start()
        elif step == 1:
            self.add(item, 3, 3)
            pl.when(self.inner)(lambda: self.reduce(item, 6).start())
            pl.when(self.outer)(lambda: self.reduce(item, 7).start())
        elif step == 2:
            self.add(item, 2, 2)
            self.reduce(item, 4).start()
        else:
            self.add(item, 1, 1)
            pl.when(self.inner)(lambda: self.add(item, 1, 7))
            self.reduce(item, 5).start()

    def sum_own(self, item, out):
        for k in (0, 4):
            self.reduce(item, k).wait_recv()
        lanes = item[4]
        for i, (own, one, two) in enumerate(
            zip(self.own(item, 0), self.came(item, 0), self.came(item, 4), strict=True)
        ):
            out[:, i * lanes : (i + 1) * lanes] = own[...].astype(F32) + one + two

    def sum_other(self, item, out):
        self.reduce(item, 5).wait_recv()
        lanes = item[4]
        for i, came in enumerate(self.came(item, 5)):
            out[:, i * lanes : (i + 1) * lanes] = came

        @pl.when(self.inner)
        def _():
            self.reduce(item, 6).wait_recv()
            for i, came in enumerate(self.came(item, 6)):
                out[:, i * lanes : (i + 1) * lanes] += came

    def reduce_sends_done(self, item):
        for k in range(7):
            self.reduce(item, k).wait_send()


class Queue:
    def __init__(self):
        self.steps = []

    def add(self, tag, fn):
        self.steps.append((tag, fn))

    def run(self, count, ready=None):
        while count > 0 and self.steps:
            tag, fn = self.steps[0]
            if ready is not None and tag not in ready:
                return
            self.steps.pop(0)
            fn()
            count -= 1

    def until(self, tag):
        while any(t == tag for t, _ in self.steps):
            self.run(1)


def layer_kernel(
    n,
    x_ref,
    cot_ref,
    seg_row,
    small_ref,
    wo_in,
    wq_in,
    wk_in,
    wv_in,
    gain_in,
    ffn_in,
    dx_ref,
    sums_ref,
    out_hbm,
    ggate_hbm,
    gup_hbm,
    gdown_hbm,
    attn,
    ffn,
    other,
    attn_land,
    ffn_land,
    gate_buf,
    up_buf,
    hid_buf,
    part,
    near,
    far,
    bend,
    xa,
    nm,
    df,
    dp_buf,
    proj_s,
    res_s,
    gains,
    gsum,
    gqk,
    q_proj,
    k_proj,
    qr,
    kr,
    vb,
    att,
    probs,
    cos_s,
    sin_s,
    stage,
    kvg,
    kvg_land,
    local_sem,
    stage_sem,
    ag_send,
    ag_recv,
    rs_send,
    rs_recv,
    cg_send,
    cg_recv,
    cr_send,
    cr_recv,
    og_send,
    og_recv,
    or_send,
    or_recv,
    qg_send,
    qg_recv,
    qr_send,
    qr_recv,
    kv_send,
    kv_recv,
):
    units, _, depth, cols = ffn.shape
    rows, width = x_ref.shape
    attn_cut = ((0, HD), (HD, 2 * HD), (2 * HD, 4 * HD), (4 * HD, attn.shape[-1]))
    parts = part_views(attn, attn_cut)
    landing = part_views(attn_land, attn_cut)
    first = len(attn_cut)
    spot4 = lax.axis_index("tensor")

    def quarter_of(t):
        return attn.at[:, :, pl.ds(pl.multiple_of(2 * HD + t * 128, 128), 128)]

    gathered = list(parts)
    gathered[2] = lambda b: attn.at[
        b, :, pl.ds(pl.multiple_of(2 * HD + spot4 * 128, 128), 128)
    ]
    ring = Ring(n, gathered, ag_send, ag_recv)
    back = Ring(n, parts, rs_send, rs_recv, lambda p, slot: landing[p](slot))
    quad = Quad(part, near, far.at[0], (qg_send, qg_recv), (qr_send, qr_recv))
    octet = Octet(part, near, far, bend, (og_send, og_recv), (or_send, or_recv))
    columns = Columns(ffn, other, ffn_land, (cg_send, cg_recv), (cr_send, cr_recv))
    me, spot = quad.me, octet.block(0)
    gq_ref, gk_ref = small_ref.at[0:1], small_ref.at[1:2]
    freq_ref = small_ref.at[2:3, pl.ds(0, HD // 2)]

    def attn_cols(low, high):
        return attn[:, :, low:high].reshape(width, high - low)

    def unit_cols(u, k, count=1):
        return ffn[u, :, :, k * UNIT : (k + count) * UNIT].reshape(width, count * UNIT)

    def across_units(k, low=0, high=units):
        return jnp.concatenate([unit_cols(u, k) for u in range(low, high)], axis=1)

    mine = [
        pltpu.make_async_copy(wo_in, attn.at[ring.me, :, pl.ds(0, HD)], local_sem.at[0]),
        pltpu.make_async_copy(wq_in, attn.at[ring.me, :, pl.ds(HD, HD)], local_sem.at[4]),
        pltpu.make_async_copy(gain_in, attn.at[ring.me, :, pl.ds(4 * HD, 128)], local_sem.at[5]),
        pltpu.make_async_copy(
            ffn_in.at[pl.ds(columns.low * units, units)], ffn.at[:, ring.me], local_sem.at[1]
        ),
        pltpu.make_async_copy(x_ref, xa.at[me], local_sem.at[2]),
        pltpu.make_async_copy(
            ffn_in.at[pl.ds((1 - columns.low) * units, units)], other, local_sem.at[3]
        ),
    ]
    for copy in mine:
        copy.start()

    def quarter_copy(source):
        cols = pl.ds(pl.multiple_of(me % 2 * 128, 128), 128)
        return pltpu.make_async_copy(
            source.at[:, cols], quarter_of(me).at[ring.me], local_sem.at[6]
        )

    pl.when(me < 2)(lambda: quarter_copy(wk_in).start())
    pl.when(me > 1)(lambda: quarter_copy(wv_in).start())
    greet = [{"dp": peer} for peer in columns.mine[1:] + columns.theirs[:1]]
    greet += [{"tensor": quad.twin}, {"tensor": quad.across}]
    barrier(greet)
    for copy in mine:
        copy.wait()
    quarter_copy(wk_in).wait()
    quad.gather_start(0, xa)

    queue = Queue()
    def ring_gather_step(parts, hop, tag):
        for p in parts:
            for way in range(2):
                if 0 < hop <= ring.reach(p, way) + 1:
                    queue.add(tag, partial(ring.gather_step, p, way, hop))

    for hop in range(1, n // 2 + 1):
        ring_gather_step((2, 3, 1), hop, -1)
        ring_gather_step((0,), hop - 2, -1)
    ring_gather_step((2, 3), n // 2 + 1, -1)
    queue.add(-1, partial(quad.gather_start, 2, quarter_of))
    queue.add(-1, partial(quad.gather_relay, 0, xa))
    queue.add(-1, partial(columns.gather_step, 0, 0))
    ring_gather_step((1,), n // 2 + 1, -1)
    ring_gather_step((0,), n // 2 - 1, -1)
    queue.add(-1, partial(quad.gather_relay, 2, quarter_of))
    ring_gather_step((0,), n // 2, -3)
    for u in range(1, EARLY):
        queue.add(-3, partial(columns.gather_step, u, 0))
    ring_gather_step((0,), n // 2 + 1, -3)
    for u in range(units + 2):
        if u < units:
            queue.add(-2, partial(columns.gather_step, u, 1))
            queue.add(-2, partial(columns.gather_step, u, 2))
        if u + EARLY < units:
            queue.add(-2, partial(columns.gather_step, u + EARLY, 0))
        if 0 < u <= units:
            queue.add(-2, partial(columns.gather_step, u - 1, 3))
        if u > 1:
            queue.add(u - 2, partial(columns.gather_step, u - 2, 4))

    queue.run(AHEAD[0])
    quarter = SEGMAX // 2

    def seg_column(seg_j, half):
        cut = seg_j[:, half * quarter : (half + 1) * quarter].astype(F32)
        return jnp.transpose(jnp.broadcast_to(cut, (128, quarter)))[:, :1]

    def tables(tile, _):
        seg_j = seg_row[pl.ds(tile, 1), :]
        for half in range(2):
            r = 2 * tile + half
            same = seg_column(seg_j, half) == seg_j.astype(F32)
            j = lax.broadcasted_iota(jnp.int32, (quarter, SEGMAX), 1)
            start = jnp.min(jnp.where(same, j, SEGMAX).astype(F32), axis=1, keepdims=True)
            i = lax.broadcasted_iota(jnp.int32, (quarter, 1), 0).astype(F32) + half * quarter
            angle = (i - start) * freq_ref[...]
            cos_s[r] = jnp.cos(angle)
            sin_s[r] = jnp.sin(angle)
        return 0

    lax.fori_loop(0, N_TILES, tables, 0)
    queue.until(-1)
    flipped = jnp.transpose(attn_cols(4 * HD, 4 * HD + 128).astype(F32))
    gains[...] = flipped[:8]
    quad.gather_end(0, xa)
    queue.run(AHEAD[2])

    sub = 32
    per = rows // sub

    def normalize(i, _):
        b, at = i // per, pl.ds(pl.multiple_of(i % per * sub, sub), sub)
        values = xa[b, at].astype(F32)
        xa[b, at] = (values * inverse_rms(values) * gains[0:1, :]).astype(BF)
        return 0

    lax.fori_loop(0, 4 * per, normalize, 0)

    def rope(values, gain_vec, r):
        normed = values * inverse_rms(values) * gain_vec
        low, high = normed[:, : HD // 2], normed[:, HD // 2 :]
        cosine, sine = cos_s[r], sin_s[r]
        return jnp.concatenate([low * cosine - high * sine, high * cosine + low * sine], axis=1)

    queue.run(AHEAD[3])

    quad.gather_end(2, quarter_of)

    def project(r, _):
        block = xa[r]
        query = dot_nn(block, attn_cols(HD, 2 * HD))
        q_proj[r] = query.astype(BF)
        qr[r] = rope(query, gq_ref[...], r).astype(BF)
        key = dot_nn(block, attn_cols(2 * HD, 3 * HD))
        k_proj[r] = key.astype(BF)
        kr[r] = rope(key, gk_ref[...], r).astype(BF)
        vb[r] = dot_nn(block, attn_cols(3 * HD, 4 * HD)).astype(BF)
        return 0

    lax.fori_loop(0, 4, project, 0)
    queue.run(AHEAD[4])

    def attend_tile(tile, _):
        two = pl.ds(2 * tile, 2)
        keys = kr[two].reshape(SEGMAX, HD)
        values = vb[two].reshape(SEGMAX, HD)
        seg_j = seg_row[pl.ds(tile, 1), :]
        for half in range(2):
            r = 2 * tile + half
            scores = dot_nt(qr[r], keys) * SCALE
            j = lax.broadcasted_iota(jnp.int32, (quarter, SEGMAX), 1)
            i = lax.broadcasted_iota(jnp.int32, (quarter, SEGMAX), 0) + half * quarter
            seen = (seg_column(seg_j, half) == seg_j.astype(F32)) & (i >= j)
            scores = jnp.where(seen, scores, NEG_LARGE)
            powers = jnp.exp(scores - jnp.max(scores, axis=1, keepdims=True))
            weights = (powers / jnp.sum(powers, axis=1, keepdims=True)).astype(BF)
            probs[r] = weights
            att[r] = dot_nn(weights, values).astype(BF)
        return 0

    lax.fori_loop(0, N_TILES, attend_tile, 0)
    queue.run(AHEAD[5])

    queue.until(-3)

    def out_block(r, _):
        part[r] = dot_nt(att[r], attn_cols(0, HD)).astype(BF)
        return 0

    lax.fori_loop(0, 4, out_block, 0)
    quad.reduce_start(0)
    queue.run(AHEAD[6])
    quad.reduce_relay(0)
    queue.run(AHEAD[7])
    quad.reduce_end(0)

    def total(at):
        return part[me, at].astype(F32) + near[0, at].astype(F32) + far[0, at].astype(F32)

    def total_ffn(at):
        return part[spot, at].astype(F32) + near[0, at].astype(F32) + (
            far[0, at].astype(F32) + far[1, at].astype(F32)
        )

    def at_rows(i):
        return pl.ds(pl.multiple_of(i * sub, sub), sub)

    def middle(i, _):
        at = at_rows(i)
        projected = total(at)
        proj_s[at] = projected.astype(BF)
        mid = x_ref[at].astype(F32) + projected * inverse_rms(projected) * gains[1:2, :]
        res_s[at] = mid
        nm[spot, at] = (mid * inverse_rms(mid) * gains[2:3, :]).astype(BF)
        return 0

    lax.fori_loop(0, per, middle, 0)
    octet.gather_start(0, nm)
    queue.run(AHEAD[8])
    octet.gather_relay(0, nm, 0)
    octet.gather_relay(0, nm, 1)
    queue.run(AHEAD[9])
    octet.gather_corner(0, nm)
    queue.run(AHEAD[9])
    octet.gather_end(0, nm)

    for u in range(units):
        queue.until(u)
        lanes = slice(u * UNIT, (u + 1) * UNIT)

        def ffn_block(r, _):
            both = dot_nn(nm[r], unit_cols(u, 0, 2))
            gate, up = both[:, :UNIT], both[:, UNIT:]
            gate_buf[r, :, lanes] = gate.astype(BF)
            up_buf[r, :, lanes] = up.astype(BF)
            hid_buf[r, :, lanes] = (gelu_parts(gate)[0] * up).astype(BF)
            return 0

        lax.fori_loop(0, 8, ffn_block, 0)
        queue.run(AHEAD[10])
    queue.run(10**6)

    def feed_block(i, _):
        b = octet.block(3 - i // 2, 1 - i % 2)
        part[b] = dot_nt(hid_buf[b], across_units(2)).astype(BF)
        octet.reduce_after(0, i)
        return 0

    lax.fori_loop(0, 8, feed_block, 0)
    for p in range(first):
        ring.gather_sends_done(p)
    for u in range(units):
        columns.gather_sends_done(u)
    octet.reduce_end(0)
    eight = (8, width)

    def fold(values):
        return jnp.sum(values.reshape(sub // 8, 8, values.shape[-1]), axis=0)

    def after_feed(i, carry):
        at = at_rows(i)
        feed = total_ffn(at)
        dx_ref[at] = (res_s[at] + feed * inverse_rms(feed) * gains[3:4, :]).astype(BF)
        grad, gain_part = rms_back(feed, gains[3:4, :], cot_ref[at].astype(F32))
        df[spot, at] = grad.astype(BF)
        return carry + fold(gain_part)

    gain_sum = lax.fori_loop(0, per, after_feed, jnp.zeros(eight, F32))
    gsum[3:4, :] = jnp.sum(gain_sum, axis=0, keepdims=True)
    put_out = pltpu.make_async_copy(dx_ref, out_hbm, local_sem.at[0])
    put_out.start()
    octet.gather_start(1, df)

    queue = Queue()
    pending = []

    def finish(item, other):
        k = len(pending)
        if k >= 2:
            for copy in pending[k - 2]:
                copy.wait()
        (columns.sum_other if other else columns.sum_own)(item, stage.at[k % 2])
        half = 1 - columns.low if other else columns.low
        unit, count, lane, lanes = item[1:]
        at = pl.multiple_of(half * (units * UNIT) + unit * UNIT, UNIT)
        outs = ((ggate_hbm, UNIT), (gup_hbm, UNIT)) if lane == 0 else ((gdown_hbm, count * UNIT),)
        copies = [
            pltpu.make_async_copy(
                stage.at[k % 2, :, pl.ds(which * UNIT, wide)],
                hbm.at[:, pl.ds(at, wide)],
                stage_sem.at[k % 2, which],
            )
            for which, (hbm, wide) in enumerate(outs)
        ]
        for copy in copies:
            copy.start()
        pending.append(copies)

    pairs = [(low, min(low + 2, units)) for low in range(0, units, 2)]
    items = [(k, low, high - low, 2 * UNIT, UNIT) for k, (low, high) in enumerate(pairs)]
    items += [(len(pairs) + u, u, 1, 0, 2 * UNIT) for u in range(units)]
    count = len(items)
    queue.add(0, partial(columns.reduce_step, items[0], 0))
    for k in range(count + 2):
        if k + 1 < count:
            queue.add(k + 1, partial(columns.reduce_step, items[k + 1], 0))
        if k < count:
            for step in range(1, 4):
                queue.add(k, partial(columns.reduce_step, items[k], step))
        if k > 1:
            queue.add(k - 2, partial(finish, items[k - 2], False))
            queue.add(k - 2, partial(finish, items[k - 2], True))
    ready = set()
    def tall(ref, lanes):
        return ref[:, :, lanes].reshape(8 * rows, lanes.stop - lanes.start)

    def down_grad(low, high):
        value = dot_tn(df[...].reshape(8 * rows, width), tall(hid_buf, slice(low * UNIT, high * UNIT)))
        value = value.astype(BF)
        for u in range(low, high):
            piece = value[:, (u - low) * UNIT : (u - low + 1) * UNIT]
            ffn[u, :, :, 2 * UNIT :] = piece.reshape(n, depth, UNIT)
        ready.add(low // 2)

    def back_block(j, _):
        octet.gather_before(1, df, j)
        b = octet.block(*octet.arrival(j))
        for low, high in pairs:
            lanes = slice(low * UNIT, high * UNIT)
            grad = dot_nn(df[b], across_units(2, low, high))
            gate, up = gate_buf[b, :, lanes].astype(F32), up_buf[b, :, lanes].astype(F32)
            act, bent = gelu_parts(gate)
            slope = 0.5 * (1.0 + bent) + 0.5 * gate * (1.0 - bent * bent) * ROOT * (
                1.0 + 3.0 * CUBIC * gate * gate
            )
            gate_buf[b, :, lanes] = (grad * up * slope).astype(BF)
            up_buf[b, :, lanes] = (grad * act).astype(BF)
        return 0

    lax.fori_loop(0, 8, back_block, 0)
    octet.gather_sends_done(1, df)

    def down_grads(some):
        for low, high in some:
            down_grad(low, high)
            queue.run(PACE[0], ready)

    down_grads(pairs[: WORK[3]])

    def back_part(i, _):
        b = octet.block(3 - i // 2, 1 - i % 2)
        grown = dot_nt(gate_buf[b], across_units(0)) + dot_nt(up_buf[b], across_units(1))
        part[b] = grown.astype(BF)
        octet.reduce_after(1, i)
        return 0

    def gate_grad(u, _):
        lanes = pl.ds(pl.multiple_of(u * UNIT, UNIT), UNIT)
        both = jnp.concatenate(
            [ref[:, :, lanes].reshape(8 * rows, UNIT) for ref in (gate_buf, up_buf)], axis=1
        )
        value = dot_tn(nm[...].reshape(8 * rows, width), both)
        ffn[u, :, :, : 2 * UNIT] = value.astype(BF).reshape(n, depth, 2 * UNIT)
        return 0

    done = [0]

    def do_work(count):
        low, done[0] = done[0], min(units, done[0] + count)
        if low < done[0]:
            lax.fori_loop(low, done[0], gate_grad, 0)
            ready.update(range(len(pairs) + low, len(pairs) + done[0]))
            queue.run(PACE[1] * (done[0] - low), ready)

    lax.fori_loop(0, 4, back_part, 0)
    queue.run(2 * PACE[0], ready)
    lax.fori_loop(4, 8, back_part, 0)
    down_grads(pairs[WORK[3] :])
    do_work(WORK[0])
    do_work(WORK[1])
    queue.run(PACE[2], ready)
    octet.reduce_end(1)

    def after_ffn(i, carry):
        at = at_rows(i)
        grad, pre_part = rms_back(res_s[at], gains[2:3, :], total_ffn(at))
        grad = cot_ref[at].astype(F32) + grad
        res_s[at] = grad
        grad, attn_part = rms_back(proj_s[at].astype(F32), gains[1:2, :], grad)
        dp_buf[me, at] = grad.astype(BF)
        return carry[0] + fold(pre_part), carry[1] + fold(attn_part)

    zero = jnp.zeros(eight, F32)
    pre_sum, attn_sum = lax.fori_loop(0, per, after_ffn, (zero, zero))
    gsum[2:3, :] = jnp.sum(pre_sum, axis=0, keepdims=True)
    gsum[1:2, :] = jnp.sum(attn_sum, axis=0, keepdims=True)
    quad.gather_start(1, dp_buf)
    do_work(WORK[2])
    queue.run(PACE[3], ready)
    quad.gather_relay(1, dp_buf)
    do_work(units)
    queue.run(PACE[4], ready)
    quad.gather_end(1, dp_buf)

    d_q, d_k, d_v = (gate_buf.at[pl.ds(0, 4), :, pl.ds(k * HD, HD)] for k in range(3))
    datt = up_buf.at[pl.ds(0, 4), :, pl.ds(0, HD)]

    def attn_grad(low, left, right):
        value = dot_tn(left.reshape(4 * rows, width), right.reshape(4 * rows, HD))
        attn[:, :, low : low + HD] = value.astype(BF).reshape(n, width // n, HD)

    def ring_hop(hop, *some):
        for p in some:
            for way in range(2):
                back.reduce_step(p, way, hop)

    ready.add(-1)
    def back_out(r, _):
        datt[r] = dot_nn(dp_buf[r], attn_cols(0, HD)).astype(BF)
        return 0

    lax.fori_loop(0, 4, back_out, 0)
    attn_grad(0, dp_buf[...], att[...])
    ring_hop(1, 0)
    queue.run(PACE[5], ready)
    gqk[...] = jnp.zeros_like(gqk)

    def unrope(grad, projection, gain_vec, r, row):
        low, high = grad[:, : HD // 2], grad[:, HD // 2 :]
        cosine, sine = cos_s[r], sin_s[r]
        grad = jnp.concatenate([low * cosine + high * sine, high * cosine - low * sine], axis=1)
        grad, gain_part = rms_back(projection, gain_vec, grad)
        gqk[row : row + 1, :] += jnp.sum(gain_part, axis=0, keepdims=True)
        return grad.astype(BF)

    def back_tile(tile, _):
        two = pl.ds(2 * tile, 2)
        keys = kr[two].reshape(SEGMAX, HD)
        values = vb[two].reshape(SEGMAX, HD)
        d_key = jnp.zeros((SEGMAX, HD), F32)
        d_value = jnp.zeros((SEGMAX, HD), F32)
        for half in range(2):
            r = 2 * tile + half
            d_att = datt[r]
            weights = probs[r]
            d_value = d_value + dot_tn(weights, d_att)
            d_probs = dot_nt(d_att, values)
            weights = weights.astype(F32)
            delta = jnp.sum(weights * d_probs, axis=1, keepdims=True)
            d_scores = (weights * (d_probs - delta) * SCALE).astype(BF)
            d_key = d_key + dot_tn(d_scores, qr[r])
            d_query = dot_nn(d_scores, keys)
            d_q[r] = unrope(d_query, q_proj[r].astype(F32), gq_ref[...], r, 4)
        for half in range(2):
            r = 2 * tile + half
            cut = slice(half * quarter, (half + 1) * quarter)
            d_k[r] = unrope(d_key[cut], k_proj[r].astype(F32), gk_ref[...], r, 5)
            d_v[r] = d_value[cut].astype(BF)
        return 0

    lax.fori_loop(0, N_TILES, back_tile, 0)
    ring_hop(2, 0)
    queue.run(PACE[5], ready)

    def back_in(r, _):
        grown = dot_nt(d_q[r], attn_cols(HD, 2 * HD))
        grown = grown + dot_nt(d_k[r], attn_cols(2 * HD, 3 * HD))
        grown = grown + dot_nt(d_v[r], attn_cols(3 * HD, 4 * HD))
        part[r] = grown.astype(BF)
        return 0

    lax.fori_loop(0, 4, back_in, 0)
    quad.reduce_start(1)
    ring_hop(3, 0)
    queue.run(PACE[5], ready)

    def three_grads(k, _):
        grad = gate_buf[0:4, :, pl.ds(pl.multiple_of(k * HD, HD), HD)]
        value = dot_tn(xa[...].reshape(4 * rows, width), grad.reshape(4 * rows, HD))
        low = pl.multiple_of((k + 1) * HD, HD)
        attn[:, :, pl.ds(low, HD)] = value.astype(BF).reshape(n, depth, HD)
        return 0

    lax.fori_loop(0, 3, three_grads, 0)
    def input_gain(i, carry):
        b, at = i // per, pl.ds(pl.multiple_of(i % per * sub, sub), sub)
        return carry + fold(part[b, at].astype(F32) * xa[b, at].astype(F32))

    gain_sum = lax.fori_loop(0, 4 * per, input_gain, zero)
    gsum[0:1, :] = jnp.sum(gain_sum, axis=0, keepdims=True) / gains[0:1, :]
    gsum[4:8, :] = jnp.zeros((4, width), F32)
    long = jnp.concatenate([gsum[...], jnp.zeros((120, width), F32)], axis=0)
    long = jnp.transpose(long).reshape(n, width // n, 128)
    short = jnp.concatenate([gqk[...], jnp.zeros((120, HD), F32)], axis=0)
    short = jnp.transpose(short).reshape(n, HD // n, 128)
    attn[:, :, 4 * HD : 4 * HD + 128] = long.astype(BF)
    attn[:, : HD // n, 4 * HD : 4 * HD + 128] = (long[:, : HD // n] + short).astype(BF)

    ring_hop(1, 2, 1, 3)
    ring_hop(4, 0)
    quad.reduce_relay(1)
    queue.run(PACE[6], ready)
    for hop in range(2, n // 2 + 1):
        ring_hop(hop, 2, 1, 3)
        queue.run(PACE[7], ready)
    quad.reduce_end(1)
    put_out.wait()

    def after_attn(i, _):
        at = at_rows(i)
        grad, _ = rms_back(x_ref[at].astype(F32), gains[0:1, :], total(at))
        dx_ref[at] = (res_s[at] + grad).astype(BF)
        return 0

    lax.fori_loop(0, per, after_attn, 0)
    queue.run(10**6)
    for p in range(2):
        sums_ref[:, p * HD : (p + 1) * HD] = back.reduce_end(p)
    kvg[0, :, : 2 * HD] = back.reduce_end(2).astype(BF)
    kvg[0, :, 2 * HD :] = back.reduce_end(3).astype(BF)
    for k, peer in enumerate((quad.twin, quad.across)):
        copy = pltpu.make_async_remote_copy(
            kvg.at[k],
            kvg_land.at[k],
            kv_send.at[k],
            kv_recv.at[k],
            device_id={"tensor": peer},
            device_id_type=MESH,
        )
        copy.start()
        copy.wait()
        grown = kvg[k].astype(F32) + kvg_land[k].astype(F32)
        if k == 0:
            kvg[1] = grown.astype(BF)
        else:
            sums_ref[:, 2 * HD :] = grown
    for p in range(len(parts)):
        back.reduce_sends_done(p)
    for item in items:
        columns.reduce_sends_done(item)
    for copies in pending[-2:]:
        for copy in copies:
            copy.wait()


AHEAD = (14, 0, 0, 2, 3, 3, 0, 6, 5, 4, 2)
PACE = (2, 2, 6, 6, 4, 3, 2, 3)
WORK = (2, 3, 2, 2)
EARLY = 3
UNIT = 128
N_TILES = 2


def run_layer(n, x, cot, segments, small, attn_weights, ffn_pack):
    rows, width = x.shape
    both, depth, cols = ffn_pack.shape
    units = both // 2
    tokens = segments.shape[0]
    wide = 4 * HD + 128
    parts = 4
    vmem, dma = pltpu.VMEM, pltpu.SemaphoreType.DMA
    grown = both * UNIT
    return pl.pallas_call(
        partial(layer_kernel, n),
        out_shape=(
            jax.ShapeDtypeStruct((rows, width), BF),
            jax.ShapeDtypeStruct((depth, wide), F32),
            jax.ShapeDtypeStruct((rows, width), BF),
            jax.ShapeDtypeStruct((depth, grown), F32),
            jax.ShapeDtypeStruct((depth, grown), F32),
            jax.ShapeDtypeStruct((depth, grown), F32),
        ),
        in_specs=vmem_specs(4) + any_specs(6),
        out_specs=vmem_specs(2) + any_specs(4),
        scratch_shapes=[
            vmem((n, depth, wide), BF),
            vmem((units, n, depth, cols), BF),
            vmem((units, depth, cols), BF),
            vmem((n - 1, depth, wide), BF),
            vmem((units, 8, depth, cols), BF),
            vmem((8, rows, units * UNIT), BF),
            vmem((8, rows, units * UNIT), BF),
            vmem((8, rows, units * UNIT), BF),
            vmem((8, rows, width), BF),
            vmem((4, rows, width), BF),
            vmem((2, rows, width), BF),
            vmem((2, rows // 2, width), BF),
            vmem((4, rows, width), BF),
            vmem((8, rows, width), BF),
            vmem((8, rows, width), BF),
            vmem((4, rows, width), BF),
            vmem((rows, width), BF),
            vmem((rows, width), F32),
            vmem((8, width), F32),
            vmem((8, width), F32),
            vmem((8, HD), F32),
            vmem((4, rows, HD), BF),
            vmem((4, rows, HD), BF),
            vmem((4, rows, HD), BF),
            vmem((4, rows, HD), BF),
            vmem((4, rows, HD), BF),
            vmem((4, rows, HD), BF),
            vmem((4, rows, SEGMAX), BF),
            vmem((4, rows, HD // 2), F32),
            vmem((4, rows, HD // 2), F32),
            vmem((2, depth, 2 * UNIT), F32),
            vmem((2, depth, wide - 2 * HD), BF),
            vmem((2, depth, wide - 2 * HD), BF),
            dma((7,)),
            dma((2, 3)),
            dma((parts, 2, n // 2)),
            dma((parts, 2, n // 2)),
            dma((parts, 2, n // 2)),
            dma((parts, 2, n // 2)),
            dma((units, 8)),
            dma((units, 8)),
            dma((units + (units + 1) // 2, 8)),
            dma((units + (units + 1) // 2, 8)),
            dma((2, 8)),
            dma((2, 8)),
            dma((2, 8)),
            dma((2, 8)),
            dma((3, 3)),
            dma((3, 3)),
            dma((2, 3)),
            dma((2, 3)),
            dma((2,)),
            dma((2,)),
        ],
        compiler_params=pltpu.CompilerParams(
            collective_id=2, has_side_effects=True, vmem_limit_bytes=67043328
        ),
    )(
        x,
        cot,
        segments.reshape(N_TILES, SEGMAX),
        small,
        *attn_weights,
        ffn_pack,
    )


def fused_local(
    inputs, segments, w_query, w_key, w_value, w_out, g_in, g_attn, g_query, g_key,
    w_gate, w_up, w_down, g_pre, g_post, cotangent,
):
    n = lax.axis_size("dp")
    depth = w_query.shape[0]
    width = w_gate.shape[1]
    lane = lax.broadcasted_iota(jnp.int32, (depth, 128), 1)
    gains = jnp.zeros((depth, 128), BF)
    for k, gain in enumerate((g_in, g_attn, g_pre, g_post)):
        gains = jnp.where(lane == k, gain[:, None], gains)
    exponent = -2.0 * (jnp.arange(HD) % (HD // 2)).astype(F32) / HD
    freq = jnp.power(jnp.float32(THETA), exponent)
    line = lax.broadcasted_iota(jnp.int32, (3, HD), 0)
    small = jnp.where(line == 0, g_query.astype(F32)[None, :], freq[None, :])
    small = jnp.where(line == 1, g_key.astype(F32)[None, :], small)
    ffn_pack = pack_ffn(w_gate, w_up, w_down.T, depth, UNIT)
    d_inputs, sums, output, g_gate, g_up, g_down = run_layer(
        n, inputs, cotangent, segments, small, (w_out.T, w_query, w_key, w_value, gains), ffn_pack
    )
    spot = lax.axis_index("tensor")
    part = depth // 4
    mine = lax.dynamic_slice_in_dim(sums[:, 2 * HD :], spot * part, part, 0)
    small = HD // n // 4
    few = lax.dynamic_slice_in_dim(sums[:, 4 * HD :], spot * small, small, 0)
    return (
        output,
        d_inputs,
        sums[:, HD : 2 * HD],
        mine[:, :HD],
        mine[:, HD : 2 * HD],
        sums[:, :HD].T,
        mine[:, 2 * HD],
        mine[:, 2 * HD + 1],
        few[:, 4],
        few[:, 5],
        g_gate[:, :width],
        g_up[:, :width],
        g_down[:, :width].T,
        mine[:, 2 * HD + 2],
        mine[:, 2 * HD + 3],
    )


def fits(mesh, depth, tokens, rows):
    return mesh.shape["dp"] == 8 and depth % 16 == 0 and mesh.shape["tensor"] == 4 and tokens == 2 * SEGMAX


def layer(mesh):
    def body(*args):
        inputs, segments, w_query = args[0], args[1], args[2]
        if fits(mesh, w_query.shape[0], segments.shape[0], inputs.shape[0]):
            return fused_local(*args)
        return local(*args)

    return body


def solution(mesh):
    return jax.shard_map(
        layer(mesh),
        mesh=mesh,
        in_specs=(
            P(("dp", "tensor"), None),
            P("dp"),
            P("dp", "tensor"),
            P("dp", None),
            P("dp", None),
            P("tensor", "dp"),
            P("dp"),
            P("dp"),
            P(),
            P(),
            P("dp", "tensor"),
            P("dp", "tensor"),
            P("tensor", "dp"),
            P("dp"),
            P("dp"),
            P(("dp", "tensor"), None),
        ),
        out_specs=(
            P(("dp", "tensor"), None),
            P(("dp", "tensor"), None),
            P("dp", "tensor"),
            P(("dp", "tensor"), None),
            P(("dp", "tensor"), None),
            P("tensor", "dp"),
            P(("dp", "tensor")),
            P(("dp", "tensor")),
            P(("dp", "tensor")),
            P(("dp", "tensor")),
            P("dp", "tensor"),
            P("dp", "tensor"),
            P("tensor", "dp"),
            P(("dp", "tensor")),
            P(("dp", "tensor")),
        ),
        check_vma=False,
    )
```

profile of v0, /device:TPU:0, one launch (start us, length us, event | category | flops | bytes accessed | tf_op | source)
XLA Modules:
  0.0 333.3 jit_solution(5473249974585037866)
XLA Ops:
  0.6 0.0 copy-start.5
  0.7 1.5 select_select_fusion.gain_in
  2.2 1.4 bitcast_bitcast_fusion
  3.6 0.0 copy-done.5
  3.6 0.1 bitcast_bitcast_fusion.2
  3.7 0.0 copy-start.7
  3.7 0.0 copy-start.8
  3.7 0.0 copy-start.6
  3.7 1.4 pad_maximum_fusion.ffn_in
  5.1 0.7 select_select_fusion.1.small_ref
  5.8 0.6 reshape.60.seg_row
  6.4 316.3 %shard_map.271 = (bf16[256,1152]{1,0:T(8,128)(2,1)}, f32[144,1152]{1,0:T(8,128)}, bf16[256,1152]{1,0:T(8,128)(2,1)}, f32[144,1792]{1,0:T(8,128)}, f32[144,1792]{1,0:T(8,128)}, /*index=5*/f32[144,1792]{1,0:T(8,128)}) custom-call(bf16[256,1152]{1,0:T(8,128)(2,1)} %x_ref.1, bf16[256,1152]{1,0:T(8,128)(2,1)} %cot_ref.1, s32[2,512]{1,0:T(2,128)} %reshape.60.seg_row, ...), custom_call_target="tpu_custom_call" | custom-call | tf_op jit(solution)/shard_map/pallas_call | solution.py:1578
  322.8 1.1 slice.46
  323.9 0.8 dynamic-slice_reduce_fusion
  324.6 0.7 fusion.3
  325.3 0.9 slice.52
  326.2 0.7 slice_reduce_fusion
  327.0 1.7 slice_bitcast_fusion.1
  328.7 0.0 copy-done.2
  328.7 1.0 slice_bitcast_fusion
  329.7 0.8 copy.44
  330.5 0.8 copy.45
  331.4 1.0 copy.46
  332.3 1.0 copy.47
  (19 shorter events, 0.1 us)
Async XLA Ops:
  0.6 2.9 copy-start.5
  3.7 1.4 copy-start.7
  3.7 1.4 copy-start.8
  3.7 2.1 copy-start.6
  322.8 5.9 %copy-start.2 = (f32[144,1792]{1,0:T(8,128)S(1)}, f32[144,1792]{1,0:T(8,128)}, u32[]{:S(2)}) copy-start(f32[144,1792]{1,0:T(8,128)} %get-tuple-element.26) | copy-start | bytes 3096580
  323.9 5.8 %copy-start.4 = (bf16[256,1152]{1,0:T(8,128)(2,1)S(1)}, bf16[256,1152]{1,0:T(8,128)(2,1)}, u32[]{:S(2)}) copy-start(bf16[256,1152]{1,0:T(8,128)(2,1)} %get-tuple-element.60) | copy-start | bytes 1769476
  328.7 1.9 copy-start.3
  329.7 1.6 copy-start.1
  330.5 1.8 copy-start
where the time goes:
time: 334 us; the launch traced here: 333 us
  Pallas kernels  316 us (95%)
  local copies, waits for them, and re-layouts  12.6 us (4%)
  other arithmetic  3.58 us (1%)
    pallas_call x1, Pallas kernels, run_layer(): pl.pallas_call(partial(layer_kernel, n), out_shape=(jax.ShapeDtypeStruct(...  316 us

commit v1 on v0

--- a/solution.py
+++ b/solution.py
@@ -1474,7 +1474,6 @@
         return 0
 
     lax.fori_loop(0, N_TILES, back_tile, 0)
-    ring_hop(2, 0)
     queue.run(PACE[5], ready)
 
     def back_in(r, _):
@@ -1486,7 +1485,6 @@
 
     lax.fori_loop(0, 4, back_in, 0)
     quad.reduce_start(1)
-    ring_hop(3, 0)
     queue.run(PACE[5], ready)
 
     def three_grads(k, _):
@@ -1511,13 +1509,29 @@
     attn[:, :, 4 * HD : 4 * HD + 128] = long.astype(BF)
     attn[:, : HD // n, 4 * HD : 4 * HD + 128] = (long[:, : HD // n] + short).astype(BF)
 
-    ring_hop(1, 2, 1, 3)
-    ring_hop(4, 0)
+    ring_hop(1, 2, 3, 1)
     quad.reduce_relay(1)
+    ring_hop(2, 0)
     queue.run(PACE[6], ready)
     for hop in range(2, n // 2 + 1):
-        ring_hop(hop, 2, 1, 3)
+        ring_hop(hop, 2, 3, 1)
+        if hop < n // 2:
+            ring_hop(hop + 1, 0)
         queue.run(PACE[7], ready)
+    kvg[0, :, : 2 * HD] = back.reduce_end(2).astype(BF)
+    kvg[0, :, 2 * HD :] = back.reduce_end(3).astype(BF)
+
+    def swap(k):
+        return pltpu.make_async_remote_copy(
+            kvg.at[k],
+            kvg_land.at[k],
+            kv_send.at[k],
+            kv_recv.at[k],
+            device_id={"tensor": (quad.twin, quad.across)[k]},
+            device_id_type=MESH,
+        )
+
+    swap(0).start()
     quad.reduce_end(1)
     put_out.wait()
 
@@ -1527,28 +1541,15 @@
         dx_ref[at] = (res_s[at] + grad).astype(BF)
         return 0
 
+    swap(0).wait()
+    kvg[1] = (kvg[0].astype(F32) + kvg_land[0].astype(F32)).astype(BF)
+    swap(1).start()
     lax.fori_loop(0, per, after_attn, 0)
     queue.run(10**6)
     for p in range(2):
         sums_ref[:, p * HD : (p + 1) * HD] = back.reduce_end(p)
-    kvg[0, :, : 2 * HD] = back.reduce_end(2).astype(BF)
-    kvg[0, :, 2 * HD :] = back.reduce_end(3).astype(BF)
-    for k, peer in enumerate((quad.twin, quad.across)):
-        copy = pltpu.make_async_remote_copy(
-            kvg.at[k],
-            kvg_land.at[k],
-            kv_send.at[k],
-            kv_recv.at[k],
-            device_id={"tensor": peer},
-            device_id_type=MESH,
-        )
-        copy.start()
-        copy.wait()
-        grown = kvg[k].astype(F32) + kvg_land[k].astype(F32)
-        if k == 0:
-            kvg[1] = grown.astype(BF)
-        else:
-            sums_ref[:, 2 * HD :] = grown
+    swap(1).wait()
+    sums_ref[:, 2 * HD :] = kvg[1].astype(F32) + kvg_land[1].astype(F32)
     for p in range(len(parts)):
         back.reduce_sends_done(p)
     for item in items:

time: 334 us -> 327 us (0.979)
  Pallas kernels: 316 us -> 307 us
    pallas_call x1, Pallas kernels: 316 us -> 307 us  [run_layer(): pl.pallas_call(partial(layer_kernel, n), out_shape=(jax.ShapeDtypeStruct(...]
where the time goes in v1:
time: 327 us; the launch traced here: 324 us
  Pallas kernels  307 us (94%)
  local copies, waits for them, and re-layouts  12.6 us (4%)
  other arithmetic  3.58 us (1%)
    pallas_call x1, Pallas kernels, run_layer(): pl.pallas_call(partial(layer_kernel, n), out_shape=(jax.ShapeDtypeStruct(...  307 us

profile of v1, /device:TPU:0, one launch (start us, length us, event | category | flops | bytes accessed | tf_op | source)
XLA Modules:
  0.0 324.4 jit_solution(14269249069616680529)
XLA Ops:
  0.7 1.5 select_select_fusion.gain_in
  2.2 1.4 bitcast_bitcast_fusion
  3.6 0.0 copy-done.5
  3.6 0.1 bitcast_bitcast_fusion.2
  3.7 0.0 copy-start.7
  3.7 0.0 copy-start.8
  3.7 0.0 copy-start.6
  3.7 1.4 pad_maximum_fusion.ffn_in
  5.1 0.0 copy-done.7
  5.1 0.7 select_select_fusion.1.small_ref
  5.8 0.0 copy-done.6
  5.8 0.6 reshape.60.seg_row
  6.4 307.4 %shard_map.271 = (bf16[256,1152]{1,0:T(8,128)(2,1)}, f32[144,1152]{1,0:T(8,128)}, bf16[256,1152]{1,0:T(8,128)(2,1)}, f32[144,1792]{1,0:T(8,128)}, f32[144,1792]{1,0:T(8,128)}, /*index=5*/f32[144,1792]{1,0:T(8,128)}) custom-call(bf16[256,1152]{1,0:T(8,128)(2,1)} %x_ref.1, bf16[256,1152]{1,0:T(8,128)(2,1)} %cot_ref.1, s32[2,512]{1,0:T(2,128)} %reshape.60.seg_row, ...), custom_call_target="tpu_custom_call" | custom-call | tf_op jit(solution)/shard_map/pallas_call | solution.py:1579
  313.8 1.1 slice.46
  315.0 0.8 dynamic-slice_reduce_fusion
  315.7 0.7 fusion.3
  316.4 0.9 slice.52
  317.3 0.7 slice_reduce_fusion
  318.0 1.7 slice_bitcast_fusion.1
  319.8 1.0 slice_bitcast_fusion
  320.8 0.8 copy.44
  321.6 0.8 copy.45
  322.4 1.0 copy.46
  323.4 1.0 copy.47
  (19 shorter events, 0.1 us)
Async XLA Ops:
  0.6 2.9 copy-start.5
  3.7 1.4 copy-start.7
  3.7 1.4 copy-start.8
  3.7 2.1 copy-start.6
  313.8 5.9 %copy-start.2 = (f32[144,1792]{1,0:T(8,128)S(1)}, f32[144,1792]{1,0:T(8,128)}, u32[]{:S(2)}) copy-start(f32[144,1792]{1,0:T(8,128)} %get-tuple-element.26) | copy-start | bytes 3096580
  314.9 5.8 %copy-start.4 = (bf16[256,1152]{1,0:T(8,128)(2,1)S(1)}, bf16[256,1152]{1,0:T(8,128)(2,1)}, u32[]{:S(2)}) copy-start(bf16[256,1152]{1,0:T(8,128)(2,1)} %get-tuple-element.60) | copy-start | bytes 1769476
  319.8 1.9 copy-start.3
  320.8 1.6 copy-start.1
  321.6 1.8 copy-start

commit v2 on v1

--- a/solution.py
+++ b/solution.py
@@ -1140,7 +1140,7 @@
     quad.gather_end(0, xa)
     queue.run(AHEAD[2])
 
-    sub = 32
+    sub = 64
     per = rows // sub
 
     def normalize(i, _):

time: 327 us -> 326 us (level)
  no operation moved by 1% of the time
where the time goes in v2:
time: 326 us; the launch traced here: 323 us
  Pallas kernels  306 us (94%)
  local copies, waits for them, and re-layouts  12.6 us (4%)
  other arithmetic  3.58 us (1%)
    pallas_call x1, Pallas kernels, run_layer(): pl.pallas_call(partial(layer_kernel, n), out_shape=(jax.ShapeDtypeStruct(...  306 us

profile of v2, /device:TPU:0, one launch (start us, length us, event | category | flops | bytes accessed | tf_op | source)
XLA Modules:
  0.0 322.8 jit_solution(6628186279862731816)
XLA Ops:
  0.6 0.0 copy-start.5
  0.7 1.5 select_select_fusion.gain_in
  2.2 1.4 bitcast_bitcast_fusion
  3.6 0.1 bitcast_bitcast_fusion.2
  3.7 0.0 copy-start.7
  3.7 0.0 copy-start.8
  3.7 0.0 copy-start.6
  3.7 1.4 pad_maximum_fusion.ffn_in
  5.1 0.7 select_select_fusion.1.small_ref
  5.8 0.6 reshape.60.seg_row
  6.4 305.8 %shard_map.271 = (bf16[256,1152]{1,0:T(8,128)(2,1)}, f32[144,1152]{1,0:T(8,128)}, bf16[256,1152]{1,0:T(8,128)(2,1)}, f32[144,1792]{1,0:T(8,128)}, f32[144,1792]{1,0:T(8,128)}, /*index=5*/f32[144,1792]{1,0:T(8,128)}) custom-call(bf16[256,1152]{1,0:T(8,128)(2,1)} %x_ref.1, bf16[256,1152]{1,0:T(8,128)(2,1)} %cot_ref.1, s32[2,512]{1,0:T(2,128)} %reshape.60.seg_row, ...), custom_call_target="tpu_custom_call" | custom-call | tf_op jit(solution)/shard_map/pallas_call | solution.py:1579
  312.2 0.0 copy-start.2
  312.3 1.1 slice.46
  313.4 0.0 copy-start.4
  313.4 0.8 dynamic-slice_reduce_fusion
  314.1 0.7 fusion.3
  314.8 0.9 slice.52
  315.7 0.7 slice_reduce_fusion
  316.5 1.7 slice_bitcast_fusion.1
  318.2 1.0 slice_bitcast_fusion
  319.2 0.8 copy.44
  320.0 0.8 copy.45
  320.8 1.0 copy.46
  321.8 1.0 copy.47
  (19 shorter events, 0.1 us)
Async XLA Ops:
  0.6 2.9 copy-start.5
  3.7 1.4 copy-start.7
  3.7 1.4 copy-start.8
  3.7 2.1 copy-start.6
  312.2 5.9 %copy-start.2 = (f32[144,1792]{1,0:T(8,128)S(1)}, f32[144,1792]{1,0:T(8,128)}, u32[]{:S(2)}) copy-start(f32[144,1792]{1,0:T(8,128)} %get-tuple-element.26) | copy-start | bytes 3096580
  313.4 5.8 %copy-start.4 = (bf16[256,1152]{1,0:T(8,128)(2,1)S(1)}, bf16[256,1152]{1,0:T(8,128)(2,1)}, u32[]{:S(2)}) copy-start(bf16[256,1152]{1,0:T(8,128)(2,1)} %get-tuple-element.60) | copy-start | bytes 1769476
  318.2 1.9 copy-start.3
  319.2 1.6 copy-start.1
  320.0 1.8 copy-start
